TPU v7x, 256 devices: a whole 4x4x8 slice. The times are simulated.
256 devices in a mesh: batch: 8 (over x, core), cache: 32 (over y, z).
Axes of the slice: x: 4, y: 4, z: 8, core: 2. Of those that a mesh axis runs over, the one named last changes fastest.
Arguments:
- hidden_in: bfloat16 [64, 4096], P('batch'), may hold values from -6 to 6
- attn_gain: bfloat16 [4096], replicated, may hold values from 0.25 to 1.75
- w_query: bfloat16 [4096, 4096], P(None, 'cache'), may hold values from -0.09375 to 0.09375
- w_key: bfloat16 [4096, 1024], P(None, 'cache'), may hold values from -0.09375 to 0.09375
- w_value: bfloat16 [4096, 1024], P(None, 'cache'), may hold values from -0.09375 to 0.09375
- key_cache: bfloat16 [64, 4096, 1024], P('batch', 'cache'), may hold values from -400 to 400, as said below
- value_cache: bfloat16 [64, 4096, 1024], P('batch', 'cache'), may hold values from -6 to 6
- write_pos: int32 [64], P('batch'), may hold values from 0 to 12287, as said below
- cache_len: int32 [64], P('batch'), may hold values from 0 to 4095, as said below
- w_out: bfloat16 [4096, 4096], P('cache'), may hold values from -0.1875 to 0.1875
- mlp_gain: bfloat16 [4096], replicated, may hold values from 0.25 to 1.75
- w_gate: bfloat16 [4096, 7168], P(None, 'cache'), may hold values from -0.09375 to 0.09375
- w_up: bfloat16 [4096, 7168], P(None, 'cache'), may hold values from -0.09375 to 0.09375
- w_down: bfloat16 [7168, 4096], P('cache'), may hold values from -0.125 to 0.125
Outputs:
- hidden_out: bfloat16 [64, 4096], P('batch', 'cache')
Inputs may be any that keep to these rules, and one draw needn't show every extreme that they name: `key_cache`: keys of earlier tokens are finite reals. `write_pos`: positions of the new tokens; the largest value occurs in every draw. cache_len never exceeds write_pos; both 0 and 4095 occur in every draw, and many sequences attend fewer than 4095 earlier tokens.
All inputs are finite; a program needn't handle non-finite values.
Results may differ from a plain program's by a relative error of at most 0.017.
Values may be sent and summed in bfloat16 or wider, within the bound.
A program may use at most 64 MiB of HBM per device.

v0:
```python
import jax
import jax.numpy as jnp
from jax import lax
from jax.sharding import PartitionSpec as P

HEADS = 32
KV_HEADS = 8
HEAD_DIM = 128


def sent_together(arrays, axis, dim, along):
    widths = [a.shape[along] for a in arrays]
    both = jnp.concatenate(arrays, axis=along)
    out = lax.all_gather(both, axis, axis=dim, tiled=True)
    return tuple(jnp.split(out, [sum(widths[:k]) for k in range(1, len(widths))], axis=along))


def sent_to_all(x, axis):
    copies = jnp.broadcast_to(x, (lax.axis_size(axis), *x.shape))
    return lax.all_to_all(copies, axis, split_axis=0, concat_axis=0, tiled=True)


def of_everyone(x, axis):
    return sent_to_all(x, axis).max(axis=0)


def over_copies(x, axis):
    return sent_to_all(x, axis).sum(axis=0)


def cut_along(x, dim, devices):
    before, after = (x.shape[:dim], x.shape[dim + 1 :])
    return jnp.moveaxis(x.reshape(*before, devices, -1, *after), dim, 0)


def sum_at_owner(x, axis, dim):
    devices = lax.axis_size(axis)
    parts = lax.all_to_all(cut_along(x, dim, devices), axis, 0, 0, tiled=True)
    return jnp.sum(parts.astype(jnp.float32), axis=0)


def laid_out(parts, dim):
    parts = jnp.moveaxis(parts, 0, dim)
    lengths = parts.shape
    return parts.reshape(*lengths[:dim], lengths[dim] * lengths[dim + 1], *lengths[dim + 2 :])


def gather_directly(x, axis, dim):
    parts = sent_to_all(x, axis)
    return laid_out(parts, dim)


def rms_norm(values, gain):
    wide = values.astype(jnp.float32)
    spread = jnp.mean(wide * wide, axis=-1, keepdims=True)
    return (wide * lax.rsqrt(spread + 1e-05) * gain.astype(jnp.float32)).astype(jnp.bfloat16)


def rotate(heads, position):
    half = heads.shape[-1] // 2
    freq = 10000.0 ** (-(jnp.arange(half, dtype=jnp.float32) * 2.0 / heads.shape[-1]))
    angle = position.astype(jnp.float32)[:, None] * freq[None, :]
    cosine = jnp.cos(angle)[:, None, :]
    sine = jnp.sin(angle)[:, None, :]
    first = heads[..., :half]
    second = heads[..., half:]
    return jnp.concatenate(
        [first * cosine - second * sine, second * cosine + first * sine], axis=-1
    )


def per_device(
    hidden_in,
    attn_gain,
    w_query,
    w_key,
    w_value,
    key_cache,
    value_cache,
    write_pos,
    cache_len,
    w_out,
    mlp_gain,
    w_gate,
    w_up,
    w_down,
):
    seqs = hidden_in.shape[0]
    embedding_width = hidden_in.shape[1]
    ncache = lax.axis_size("cache")
    position_index = lax.axis_index("cache")
    slots_dev = key_cache.shape[1]
    window = slots_dev * ncache
    group = HEADS // KV_HEADS
    scale = 1.0 / HEAD_DIM**0.5
    feature_width = embedding_width // ncache
    normed = rms_norm(hidden_in, attn_gain)
    query_slice = jnp.dot(normed, w_query, preferred_element_type=jnp.float32).astype(jnp.bfloat16)
    key_part = jnp.dot(normed, w_key, preferred_element_type=jnp.float32).astype(jnp.bfloat16)
    value_part = jnp.dot(normed, w_value, preferred_element_type=jnp.float32).astype(jnp.bfloat16)
    query_raw, key_raw, value_new = (
        lax.all_gather(query_slice, "cache", axis=1, tiled=True),
        *sent_together((key_part, value_part), "cache", 1, 0),
    )
    query = rotate(query_raw.astype(jnp.float32).reshape(seqs, HEADS, HEAD_DIM), write_pos).astype(
        jnp.bfloat16
    )
    fresh_key_row = rotate(
        key_raw.astype(jnp.float32).reshape(seqs, KV_HEADS, HEAD_DIM), write_pos
    ).astype(jnp.bfloat16)
    value_heads = value_new.reshape(seqs, KV_HEADS, HEAD_DIM)
    slots = position_index * slots_dev + jnp.arange(slots_dev, dtype=jnp.int32)
    dist = (write_pos[:, None] - 1 - slots[None, :]) % window + 1
    valid = dist <= cache_len[:, None]
    owner = write_pos % window // slots_dev == position_index
    query_head_group = query.reshape(seqs, KV_HEADS, group, HEAD_DIM)
    keys = key_cache.reshape(seqs, slots_dev, KV_HEADS, HEAD_DIM)
    values = value_cache.reshape(seqs, slots_dev, KV_HEADS, HEAD_DIM)
    scores = (
        jnp.einsum("bkgd,bwkd->bkgw", query_head_group, keys, preferred_element_type=jnp.float32)
        * scale
    )
    own = (
        jnp.einsum(
            "vyjf,vyf->vyj", query_head_group, fresh_key_row, preferred_element_type=jnp.float32
        )
        * scale
    )
    scores = jnp.where(valid[:, None, None, :], scores, -1e30)
    own = jnp.where(owner[:, None, None], own, -1e30)
    top = jnp.maximum(jnp.max(scores, axis=-1), own)
    weights = jnp.where(valid[:, None, None, :], jnp.exp(scores - top[..., None]), 0.0)
    own_weight = jnp.where(owner[:, None, None], jnp.exp(own - top), 0.0)
    total = jnp.sum(weights, axis=-1) + own_weight
    own_low = lax.optimization_barrier(own_weight.astype(jnp.bfloat16)).astype(jnp.float32)
    reduced_total = jnp.einsum(
        "bkgw,bwkd->bkgd", weights.astype(jnp.bfloat16), values, preferred_element_type=jnp.float32
    )
    reduced_total = (
        reduced_total + own_low[..., None] * value_heads.astype(jnp.float32)[:, :, None, :]
    )
    top_flat = top.reshape(seqs, HEADS)
    total_flat = total.reshape(seqs, HEADS)
    summed_flat = reduced_total.reshape(seqs, HEADS, HEAD_DIM)
    largest = of_everyone(top_flat, "cache")
    factor = jnp.exp(top_flat - largest)
    scaled_total = over_copies(total_flat * factor, "cache")
    scaled_sum = (summed_flat * factor[..., None]).reshape(seqs, HEADS * HEAD_DIM)
    local_partial_sum = sum_at_owner(scaled_sum.astype(jnp.bfloat16), "cache", 1)
    total_features = jnp.repeat(scaled_total, HEAD_DIM, axis=1)
    own_total = lax.dynamic_slice_in_dim(
        total_features, position_index * feature_width, feature_width, 1
    )
    attended = (local_partial_sum / own_total).astype(jnp.bfloat16)
    projected = jnp.dot(attended, w_out, preferred_element_type=jnp.float32)
    share = sum_at_owner(projected.astype(jnp.bfloat16), "cache", 1)
    hidden_share = lax.dynamic_slice_in_dim(
        hidden_in, position_index * feature_width, feature_width, 1
    )
    mid_own = (hidden_share.astype(jnp.float32) + share).astype(jnp.bfloat16)
    mid_wide = mid_own.astype(jnp.float32)
    squares = over_copies(jnp.sum(mid_wide * mid_wide, axis=-1), "cache")
    gain_share = lax.dynamic_slice_in_dim(
        mlp_gain, position_index * feature_width, feature_width, 0
    )
    normed_share = (
        mid_wide
        * lax.rsqrt(squares / embedding_width + 1e-05)[:, None]
        * gain_share.astype(jnp.float32)
    ).astype(jnp.bfloat16)
    normed_mid = gather_directly(normed_share, "cache", 1)
    gate = jnp.dot(normed_mid, w_gate, preferred_element_type=jnp.float32)
    upper = jnp.dot(normed_mid, w_up, preferred_element_type=jnp.float32)
    act = (jax.nn.silu(gate) * upper).astype(jnp.bfloat16)
    down = jnp.dot(act, w_down, preferred_element_type=jnp.float32)
    down_own = sum_at_owner(down.astype(jnp.bfloat16), "cache", 1)
    return (mid_own.astype(jnp.float32) + down_own).astype(jnp.bfloat16)


def solution(mesh):
    in_specs = (
        P("batch", None),
        P(),
        P(None, "cache"),
        P(None, "cache"),
        P(None, "cache"),
        P("batch", "cache", None),
        P("batch", "cache", None),
        P("batch"),
        P("batch"),
        P("cache", None),
        P(),
        P(None, "cache"),
        P(None, "cache"),
        P("cache", None),
    )
    out_specs = P("batch", "cache")
    return jax.shard_map(
        per_device, mesh=mesh, in_specs=in_specs, out_specs=out_specs, check_vma=False
    )
```

profile of v0, /device:TPU:4, one launch (start us, length us, event | category | flops | bytes accessed | tf_op | source)
XLA Modules:
  0.0 211.6 jit_solution(16157100261924183315)
XLA Ops:
  0.0 0.8 fusion.62
  0.8 0.7 fusion.52
  1.5 1.0 fusion.18
  2.5 0.7 convert_element_type.92
  3.2 1.2 convolution_convert_fusion.3
  4.5 1.2 convolution_convert_fusion.2
  5.7 1.6 convolution_convert_fusion.4
  7.3 52.3 %all_gather.6 = bf16[8,4096]{1,0:T(8,128)(2,1)S(1)} all-gather(bf16[8,128]{1,0:T(8,128)(2,1)S(1)} %convolution_convert_fusion.4), channel_id=1, replica_groups=mesh['batch'=8,'cache'=32] {'cache'}, dimensions={1}, use_global_device_ids=true | all-gather | bytes 67584 | tf_op jit(solution)/shard_map/all_gather | solution.py:102
  59.9 42.2 %all-gather = bf16[32,32,16]{1,2,0:T(8,128)(2,1)S(1)} all-gather(bf16[1,32,16]{1,2,0:T(8,128)(2,1)S(1)} %maximum_bitcast_fusion.1), channel_id=1, replica_groups=mesh['batch'=8,'cache'=32] {'cache'}, dimensions={0}, use_global_device_ids=true | all-gather | bytes 33792 | tf_op jit(solution)/shard_map/all_gather | solution.py:14
  102.9 1.3 fusion.63
  104.5 0.7 reshape.212
  105.2 5.7 %all-to-all-start = ((f32[32,1,256]{2,1,0:T(1,128)}), f32[32,1,256]{2,1,0:T(1,128)S(1)}, u32[]{:S(2)}, u32[]{:S(2)}) async-start(f32[32,1,256]{2,1,0:T(1,128)} %reshape.212), calls=%async_computation | async-start | bytes 65536 | tf_op jit(solution)/shard_map/all_to_all | solution.py:20
  111.3 2.4 %fusion.12 = f32[8,8,4,128]{3,2,1,0:T(4,128)S(1)} fusion(f32[8,8,4,128]{3,2,1,0:T(4,128)S(1)} %get-tuple-element.22, f32[8,8,128]{2,1,0:T(8,128)S(1)} %copy.60, f32[8,8,4]{2,1,0:T(8,128)S(1)} %convert_element_type.100, f32[8,8,4]{2,1,0:T(8,128)S(1)} %fusion.35, pred[8,128]{1,0:T(8,128)(4,1)S(1)} %fusion.44, bf16[8,128,1024]{2,1,0:T(8,128)(2,1)} %param.20), kind=kOutput, calls=%fused_computation.10 | convolution fusion | flops 8552448 | bytes 2395136 | tf_op jit(solution)/shard_map/bkgw,bwkd->bkgd/dot_general | solution.py:136
  113.9 6.9 %all-to-all-done = f32[32,1,256]{2,1,0:T(1,128)S(1)} async-done(((f32[32,1,256]{2,1,0:T(1,128)}), f32[32,1,256]{2,1,0:T(1,128)S(1)}, u32[]{:S(2)}, u32[]{:S(2)}) %all-to-all-start) | async-done | bytes 32800 | tf_op jit(solution)/shard_map/all_to_all | solution.py:20
  121.4 0.7 reduce.1
  122.3 0.7 reshape.214
  123.0 3.8 %all-to-all-start.2 = ((f32[32,1,256]{2,1,0:T(1,128)}), f32[32,1,256]{2,1,0:T(1,128)S(1)}, u32[]{:S(2)}, u32[]{:S(2)}) async-start(f32[32,1,256]{2,1,0:T(1,128)} %reshape.214), calls=%async_computation.2 | async-start | bytes 65536 | tf_op jit(solution)/shard_map/all_to_all | solution.py:20
  126.8 0.7 fusion.25
  127.6 9.1 %all-to-all-done.2 = f32[32,1,256]{2,1,0:T(1,128)S(1)} async-done(((f32[32,1,256]{2,1,0:T(1,128)}), f32[32,1,256]{2,1,0:T(1,128)S(1)}, u32[]{:S(2)}, u32[]{:S(2)}) %all-to-all-start.2) | async-done | bytes 32800 | tf_op jit(solution)/shard_map/all_to_all | solution.py:20
  136.7 3.9 %all-to-all-start.1 = ((bf16[32,8,128]{2,1,0:T(8,128)(2,1)}), bf16[32,8,128]{2,1,0:T(8,128)(2,1)S(1)}, u32[]{:S(2)}, u32[]{:S(2)}) async-start(bf16[32,8,128]{2,1,0:T(8,128)(2,1)} %fusion.25), calls=%async_computation.1 | async-start | bytes 131072 | tf_op jit(solution)/shard_map/all_to_all | solution.py:38
  140.6 0.7 reduce.2
  141.6 9.0 %all-to-all-done.1 = bf16[32,8,128]{2,1,0:T(8,128)(2,1)S(1)} async-done(((bf16[32,8,128]{2,1,0:T(8,128)(2,1)}), bf16[32,8,128]{2,1,0:T(8,128)(2,1)S(1)}, u32[]{:S(2)}, u32[]{:S(2)}) %all-to-all-start.1) | async-done | bytes 65568 | tf_op jit(solution)/shard_map/all_to_all | solution.py:38
  150.9 13.2 %all_to_all.36 = bf16[32,8,128]{2,1,0:T(8,128)(2,1)S(1)} all-to-all(bf16[32,8,128]{2,1,0:T(8,128)(2,1)S(1)} %fusion.15), channel_id=1, replica_groups=mesh['batch'=8,'cache'=32] {'cache'}, dimensions={0} | all-to-all | bytes 131072 | tf_op jit(solution)/shard_map/all_to_all | solution.py:38
  164.1 0.8 fusion.45
  164.9 0.6 broadcast_in_dim.83
  165.5 3.9 %all-to-all-start.4 = ((f32[32,1,8]{2,1,0:T(1,128)}), f32[32,1,8]{2,1,0:T(1,128)S(1)}, u32[]{:S(2)}, u32[]{:S(2)}) async-start(f32[32,1,8]{2,1,0:T(1,128)} %broadcast_in_dim.83), calls=%async_computation.4 | async-start | bytes 32768 | tf_op jit(solution)/shard_map/all_to_all | solution.py:20
  169.3 0.8 dynamic-slice_convert_fusion
  170.1 9.1 %all-to-all-done.4 = f32[32,1,8]{2,1,0:T(1,128)S(1)} async-done(((f32[32,1,8]{2,1,0:T(1,128)}), f32[32,1,8]{2,1,0:T(1,128)S(1)}, u32[]{:S(2)}, u32[]{:S(2)}) %all-to-all-start.4) | async-done | bytes 1056 | tf_op jit(solution)/shard_map/all_to_all | solution.py:20
  179.3 13.0 %all_to_all.37 = bf16[32,8,128]{2,1,0:T(8,128)(2,1)S(1)} all-to-all(bf16[32,8,128]{2,1,0:T(8,128)(2,1)S(1)} %broadcast_in_dim.84), channel_id=1, replica_groups=mesh['batch'=8,'cache'=32] {'cache'}, dimensions={0} | all-to-all | bytes 131072 | tf_op jit(solution)/shard_map/all_to_all | solution.py:20
  192.3 2.1 fusion.28
  194.3 3.4 %fusion.16 = bf16[32,8,128]{2,1,0:T(8,128)(2,1)S(1)} fusion(bf16[224,4096]{1,0:T(8,128)(2,1)} %param.27, bf16[4096,224]{0,1:T(8,128)(2,1)} %param.26, bf16[32,8,128]{2,1,0:T(8,128)(2,1)S(1)} %all_to_all.37, f32[8,224]{1,0:T(8,128)S(1)} %fusion.28), kind=kOutput, calls=%fused_computation.12 | convolution fusion | flops 29403648 | bytes 3808256 | tf_op jit(solution)/shard_map/dot_general | solution.py:175
  197.8 13.2 %all_to_all.38 = bf16[32,8,128]{2,1,0:T(8,128)(2,1)S(1)} all-to-all(bf16[32,8,128]{2,1,0:T(8,128)(2,1)S(1)} %fusion.16), channel_id=1, replica_groups=mesh['batch'=8,'cache'=32] {'cache'}, dimensions={0} | all-to-all | bytes 131072 | tf_op jit(solution)/shard_map/all_to_all | solution.py:38
  (51 shorter events, 4.0 us)
Async XLA Ops:
  0.0 102.9 %copy-start = (bf16[8,128,1024]{2,1,0:T(8,128)(2,1)S(1)}, bf16[8,128,1024]{2,1,0:T(8,128)(2,1)}, u32[]{:S(2)}) copy-start(bf16[8,128,1024]{2,1,0:T(8,128)(2,1)} %param.19) | copy-start | bytes 6291460
  0.0 102.5 %copy-start.2 = (s32[8]{0:T(128)S(1)}, s32[8]{0:T(128)}, u32[]{:S(2)}) copy-start(s32[8]{0:T(128)} %param.22) | copy-start | bytes 100
  105.2 15.6 %all-to-all-start = ((f32[32,1,256]{2,1,0:T(1,128)}), f32[32,1,256]{2,1,0:T(1,128)S(1)}, u32[]{:S(2)}, u32[]{:S(2)}) async-start(f32[32,1,256]{2,1,0:T(1,128)} %reshape.212), calls=%async_computation | async-start | bytes 65536 | tf_op jit(solution)/shard_map/all_to_all | solution.py:20
  111.3 39.3 %copy-start.1 = (bf16[128,4096]{1,0:T(8,128)(2,1)S(1)}, bf16[128,4096]{1,0:T(8,128)(2,1)}, u32[]{:S(2)}) copy-start(bf16[128,4096]{1,0:T(8,128)(2,1)} %param.23) | copy-start | bytes 3145732
  123.0 13.7 %all-to-all-start.2 = ((f32[32,1,256]{2,1,0:T(1,128)}), f32[32,1,256]{2,1,0:T(1,128)S(1)}, u32[]{:S(2)}, u32[]{:S(2)}) async-start(f32[32,1,256]{2,1,0:T(1,128)} %reshape.214), calls=%async_computation.2 | async-start | bytes 65536 | tf_op jit(solution)/shard_map/all_to_all | solution.py:20
  136.7 13.9 %all-to-all-start.1 = ((bf16[32,8,128]{2,1,0:T(8,128)(2,1)}), bf16[32,8,128]{2,1,0:T(8,128)(2,1)S(1)}, u32[]{:S(2)}, u32[]{:S(2)}) async-start(bf16[32,8,128]{2,1,0:T(8,128)(2,1)} %fusion.25), calls=%async_computation.1 | async-start | bytes 131072 | tf_op jit(solution)/shard_map/all_to_all | solution.py:38
  165.5 13.7 %all-to-all-start.4 = ((f32[32,1,8]{2,1,0:T(1,128)}), f32[32,1,8]{2,1,0:T(1,128)S(1)}, u32[]{:S(2)}, u32[]{:S(2)}) async-start(f32[32,1,8]{2,1,0:T(1,128)} %broadcast_in_dim.83), calls=%async_computation.4 | async-start | bytes 32768 | tf_op jit(solution)/shard_map/all_to_all | solution.py:20
where the time goes:
time: 212 us
  blocking collectives  134 us (63%)
  waiting for transfers between devices  34.1 us (16%)
  starting transfers between devices  17.2 us (8%)
  matrix products  13.7 us (6%)
  other arithmetic  8.78 us (4%)
  local copies, waits for them, and re-layouts  3.68 us (2%)
    all_gather x1, blocking collectives, per_device(): lax.all_gather(query_slice, 'cache', axis=1, tiled=True)  52.3 us
    all_gather x1, blocking collectives, sent_together(): out = lax.all_gather(both, axis, axis=dim, tiled=True)  42.2 us
    all_to_all x2, blocking collectives, sum_at_owner(): parts = lax.all_to_all(cut_along(x, dim, devices), axis, 0, 0, tiled=True)  26.3 us
    all_to_all x3, waiting for transfers between devices, sent_to_all(): return lax.all_to_all(copies, axis, split_axis=0, concat_axis=0, tiled=True)  25.1 us
    all_to_all x3, starting transfers between devices, sent_to_all(): return lax.all_to_all(copies, axis, split_axis=0, concat_axis=0, tiled=True)  13.3 us
    all_to_all x1, blocking collectives, sent_to_all(): return lax.all_to_all(copies, axis, split_axis=0, concat_axis=0, tiled=True)  13 us
    all_to_all x1, waiting for transfers between devices, sum_at_owner(): parts = lax.all_to_all(cut_along(x, dim, devices), axis, 0, 0, tiled=True)  8.97 us
  transfers between devices with their start and end apart: 4, of which 4 were waited for; matrix products, arithmetic and copies ran while one was open for 3% of the time, Pallas kernels for 0%

commit v1 on v0

--- a/solution.py
+++ b/solution.py
@@ -98,8 +98,19 @@
     query_slice = jnp.dot(normed, w_query, preferred_element_type=jnp.float32).astype(jnp.bfloat16)
     key_part = jnp.dot(normed, w_key, preferred_element_type=jnp.float32).astype(jnp.bfloat16)
     value_part = jnp.dot(normed, w_value, preferred_element_type=jnp.float32).astype(jnp.bfloat16)
+
+    def plane_find(packet):
+        y_new = jax.lax.all_to_all(
+            jnp.concatenate(tuple((packet for _ in range(jax.lax.axis_size("cache")))), axis=1),
+            axis_name="cache",
+            split_axis=1,
+            concat_axis=1,
+            tiled=True,
+        )
+        return y_new
+
     query_raw, key_raw, value_new = (
-        lax.all_gather(query_slice, "cache", axis=1, tiled=True),
+        plane_find(query_slice),
         *sent_together((key_part, value_part), "cache", 1, 0),
     )
     query = rotate(query_raw.astype(jnp.float32).reshape(seqs, HEADS, HEAD_DIM), write_pos).astype(

time: 212 us -> 194 us (0.915)
  blocking collectives: 134 us -> 83.4 us
  local copies, waits for them, and re-layouts: 3.68 us -> 22.3 us
  starting transfers between devices: 17.2 us -> 30 us
    all_gather x1 -> x0, blocking collectives: 52.3 us -> none  [per_device(): lax.all_gather(query_slice, 'cache', axis=1, tiled=True)]
    unnamed x11 -> x43, local copies, waits for them, and re-layouts: 1.79 us -> 19.2 us
    all_to_all x0 -> x1, starting transfers between devices: none -> 11.5 us  [plane_find(): jax.lax.all_to_all(jnp.concatenate(tuple((packet for _ in range(jax.lax.a...]
  transfers between devices with their start and end apart: 4 -> 5, of which waited for: 4 -> 4; matrix products, arithmetic and copies ran while one was open for 3% -> 5% of each run, Pallas kernels for 0% -> 0%
where the time goes in v1:
time: 194 us; the launch traced here: 193 us
  blocking collectives  83.4 us (43%)
  waiting for transfers between devices  34.6 us (18%)
  starting transfers between devices  30 us (15%)
  local copies, waits for them, and re-layouts  22.3 us (11%)
  matrix products  14.3 us (7%)
  other arithmetic  8.22 us (4%)
    all_gather x1, blocking collectives, sent_together(): out = lax.all_gather(both, axis, axis=dim, tiled=True)  44.1 us
    all_to_all x2, blocking collectives, sum_at_owner(): parts = lax.all_to_all(cut_along(x, dim, devices), axis, 0, 0, tiled=True)  26.2 us
    all_to_all x3, waiting for transfers between devices, sent_to_all(): return lax.all_to_all(copies, axis, split_axis=0, concat_axis=0, tiled=True)  25.6 us
    unnamed x43, local copies, waits for them, and re-layouts  19.2 us
    all_to_all x3, starting transfers between devices, sent_to_all(): return lax.all_to_all(copies, axis, split_axis=0, concat_axis=0, tiled=True)  14.6 us
    all_to_all x1, blocking collectives, sent_to_all(): return lax.all_to_all(copies, axis, split_axis=0, concat_axis=0, tiled=True)  13.2 us
    all_to_all x1, starting transfers between devices, plane_find(): jax.lax.all_to_all(jnp.concatenate(tuple((packet for _ in range(jax.lax.a...  11.5 us
    all_to_all x1, waiting for transfers between devices, sum_at_owner(): parts = lax.all_to_all(cut_along(x, dim, devices), axis, 0, 0, tiled=True)  9.06 us
  transfers between devices with their start and end apart: 5, of which 4 were waited for; matrix products, arithmetic and copies ran while one was open for 5% of the time, Pallas kernels for 0%

profile of v1, /device:TPU:4, one launch (start us, length us, event | category | flops | bytes accessed | tf_op | source)
XLA Modules:
  0.0 193.1 jit_solution(954151615337496523)
XLA Ops:
  0.0 1.2 fusion.18
  1.2 0.7 convert_element_type.95
  1.9 2.2 %constant_dynamic-update-slice_fusion.31 = (bf16[8,4096]{1,0:T(8,128)(2,1)}, bf16[8,128]{1,0:T(8,128)(2,1)S(1)}) fusion(bf16[4096,128]{1,0:T(8,128)(2,1)} %param.16, bf16[8,4096]{1,0:T(8,128)(2,1)} %param.14, f32[4096]{0:T(1024)S(1)} %convert_element_type.95, f32[8]{0:T(128)S(1)} %add_rsqrt_fusion.1), kind=kOutput, calls=%fused_computation.64 | convolution fusion | flops 8520703 | bytes 1134624 | tf_op jit(solution)/shard_map/dot_general | solution.py:98
  22.1 11.5 %all-to-all-start = ((bf16[8,32,128]{2,0,1:T(8,128)(2,1)}), bf16[8,32,128]{2,0,1:T(8,128)(2,1)S(1)}, u32[]{:S(2)}, u32[]{:S(2)}) async-start(bf16[8,32,128]{2,0,1:T(8,128)(2,1)} %bitcast), calls=%async_computation | async-start | bytes 131072 | tf_op jit(solution)/shard_map/all_to_all | solution.py:103
  33.6 0.7 fusion.62
  34.3 1.2 convolution_convert_fusion.3
  35.6 1.2 convolution_convert_fusion.2
  36.8 44.1 %all-gather = bf16[32,32,16]{1,2,0:T(8,128)(2,1)S(1)} all-gather(bf16[1,32,16]{1,2,0:T(8,128)(2,1)S(1)} %maximum_bitcast_fusion.1), channel_id=1, replica_groups=mesh['batch'=8,'cache'=32] {'cache'}, dimensions={0}, use_global_device_ids=true | all-gather | bytes 33792 | tf_op jit(solution)/shard_map/all_gather | solution.py:14
  81.4 0.6 copy.60
  82.6 1.3 fusion.63
  84.6 0.7 reshape.205
  85.3 7.0 %all-to-all-start.1 = ((f32[32,1,256]{2,1,0:T(1,128)}), f32[32,1,256]{2,1,0:T(1,128)S(1)}, u32[]{:S(2)}, u32[]{:S(2)}) async-start(f32[32,1,256]{2,1,0:T(1,128)} %reshape.205), calls=%async_computation.1 | async-start | bytes 65536 | tf_op jit(solution)/shard_map/all_to_all | solution.py:20
  92.3 2.4 %fusion.12 = f32[8,8,4,128]{3,2,1,0:T(4,128)S(1)} fusion(f32[8,8,4,128]{3,2,1,0:T(4,128)S(1)} %get-tuple-element.24, f32[8,8,128]{2,1,0:T(8,128)} %copy.60, f32[8,8,4]{2,1,0:T(8,128)S(1)} %convert_element_type.104, f32[8,8,4]{2,1,0:T(8,128)S(1)} %fusion.35, pred[8,128]{1,0:T(8,128)(4,1)S(1)} %fusion.44, bf16[8,128,1024]{2,1,0:T(8,128)(2,1)} %param.20), kind=kOutput, calls=%fused_computation.10 | convolution fusion | flops 8552448 | bytes 2395136 | tf_op jit(solution)/shard_map/bkgw,bwkd->bkgd/dot_general | solution.py:147
  94.9 7.3 %all-to-all-done.1 = f32[32,1,256]{2,1,0:T(1,128)S(1)} async-done(((f32[32,1,256]{2,1,0:T(1,128)}), f32[32,1,256]{2,1,0:T(1,128)S(1)}, u32[]{:S(2)}, u32[]{:S(2)}) %all-to-all-start.1) | async-done | bytes 32800 | tf_op jit(solution)/shard_map/all_to_all | solution.py:20
  102.7 0.7 reduce.1
  103.7 0.7 reshape.207
  104.4 3.8 %all-to-all-start.3 = ((f32[32,1,256]{2,1,0:T(1,128)}), f32[32,1,256]{2,1,0:T(1,128)S(1)}, u32[]{:S(2)}, u32[]{:S(2)}) async-start(f32[32,1,256]{2,1,0:T(1,128)} %reshape.207), calls=%async_computation.3 | async-start | bytes 65536 | tf_op jit(solution)/shard_map/all_to_all | solution.py:20
  108.2 0.7 fusion.25
  108.9 9.2 %all-to-all-done.3 = f32[32,1,256]{2,1,0:T(1,128)S(1)} async-done(((f32[32,1,256]{2,1,0:T(1,128)}), f32[32,1,256]{2,1,0:T(1,128)S(1)}, u32[]{:S(2)}, u32[]{:S(2)}) %all-to-all-start.3) | async-done | bytes 32800 | tf_op jit(solution)/shard_map/all_to_all | solution.py:20
  118.1 3.9 %all-to-all-start.2 = ((bf16[32,8,128]{2,1,0:T(8,128)(2,1)}), bf16[32,8,128]{2,1,0:T(8,128)(2,1)S(1)}, u32[]{:S(2)}, u32[]{:S(2)}) async-start(bf16[32,8,128]{2,1,0:T(8,128)(2,1)} %fusion.25), calls=%async_computation.2 | async-start | bytes 131072 | tf_op jit(solution)/shard_map/all_to_all | solution.py:38
  122.0 0.7 reduce.2
  123.0 9.1 %all-to-all-done.2 = bf16[32,8,128]{2,1,0:T(8,128)(2,1)S(1)} async-done(((bf16[32,8,128]{2,1,0:T(8,128)(2,1)}), bf16[32,8,128]{2,1,0:T(8,128)(2,1)S(1)}, u32[]{:S(2)}, u32[]{:S(2)}) %all-to-all-start.2) | async-done | bytes 65568 | tf_op jit(solution)/shard_map/all_to_all | solution.py:38
  132.4 13.1 %all_to_all.45 = bf16[32,8,128]{2,1,0:T(8,128)(2,1)S(1)} all-to-all(bf16[32,8,128]{2,1,0:T(8,128)(2,1)S(1)} %fusion.15), channel_id=1, replica_groups=mesh['batch'=8,'cache'=32] {'cache'}, dimensions={0} | all-to-all | bytes 131072 | tf_op jit(solution)/shard_map/all_to_all | solution.py:38
  145.5 0.8 fusion.45
  146.3 0.6 broadcast_in_dim.83
  146.9 3.9 %all-to-all-start.5 = ((f32[32,1,8]{2,1,0:T(1,128)}), f32[32,1,8]{2,1,0:T(1,128)S(1)}, u32[]{:S(2)}, u32[]{:S(2)}) async-start(f32[32,1,8]{2,1,0:T(1,128)} %broadcast_in_dim.83), calls=%async_computation.5 | async-start | bytes 32768 | tf_op jit(solution)/shard_map/all_to_all | solution.py:20
  150.7 0.8 dynamic-slice_convert_fusion
  151.5 9.1 %all-to-all-done.5 = f32[32,1,8]{2,1,0:T(1,128)S(1)} async-done(((f32[32,1,8]{2,1,0:T(1,128)}), f32[32,1,8]{2,1,0:T(1,128)S(1)}, u32[]{:S(2)}, u32[]{:S(2)}) %all-to-all-start.5) | async-done | bytes 1056 | tf_op jit(solution)/shard_map/all_to_all | solution.py:20
  160.7 13.2 %all_to_all.46 = bf16[32,8,128]{2,1,0:T(8,128)(2,1)S(1)} all-to-all(bf16[32,8,128]{2,1,0:T(8,128)(2,1)S(1)} %broadcast_in_dim.84), channel_id=1, replica_groups=mesh['batch'=8,'cache'=32] {'cache'}, dimensions={0} | all-to-all | bytes 131072 | tf_op jit(solution)/shard_map/all_to_all | solution.py:20
  173.9 2.1 %fusion.28 = f32[8,224]{1,0:T(8,128)S(1)} fusion(bf16[4096,224]{0,1:T(8,128)(2,1)} %param.25, bf16[32,8,128]{2,1,0:T(8,128)(2,1)S(1)} %all_to_all.46), kind=kOutput, calls=%fused_computation.68 | convolution fusion | flops 14680064 | bytes 1907712 | tf_op jit(solution)/shard_map/dot_general | solution.py:183
  176.0 3.4 %fusion.16 = bf16[32,8,128]{2,1,0:T(8,128)(2,1)S(1)} fusion(bf16[224,4096]{1,0:T(8,128)(2,1)} %param.27, bf16[4096,224]{0,1:T(8,128)(2,1)} %param.26, bf16[32,8,128]{2,1,0:T(8,128)(2,1)S(1)} %all_to_all.46, f32[8,224]{1,0:T(8,128)S(1)} %fusion.28), kind=kOutput, calls=%fused_computation.12 | convolution fusion | flops 29403648 | bytes 3808256 | tf_op jit(solution)/shard_map/dot_general | solution.py:186
  179.4 13.1 %all_to_all.47 = bf16[32,8,128]{2,1,0:T(8,128)(2,1)S(1)} all-to-all(bf16[32,8,128]{2,1,0:T(8,128)(2,1)S(1)} %fusion.16), channel_id=1, replica_groups=mesh['batch'=8,'cache'=32] {'cache'}, dimensions={0} | all-to-all | bytes 131072 | tf_op jit(solution)/shard_map/all_to_all | solution.py:38
  (85 shorter events, 22.0 us)
Async XLA Ops:
  0.0 82.5 %copy-start = (bf16[8,128,1024]{2,1,0:T(8,128)(2,1)S(1)}, bf16[8,128,1024]{2,1,0:T(8,128)(2,1)}, u32[]{:S(2)}) copy-start(bf16[8,128,1024]{2,1,0:T(8,128)(2,1)} %param.19) | copy-start | bytes 6291460
  0.0 81.4 %copy-start.3 = (s32[8]{0:T(128)S(1)}, s32[8]{0:T(128)}, u32[]{:S(2)}) copy-start(s32[8]{0:T(128)} %param.21) | copy-start | bytes 100
  0.0 81.2 %copy-start.2 = (s32[8]{0:T(128)S(1)}, s32[8]{0:T(128)}, u32[]{:S(2)}) copy-start(s32[8]{0:T(128)} %param.22) | copy-start | bytes 100
  22.1 60.0 %all-to-all-start = ((bf16[8,32,128]{2,0,1:T(8,128)(2,1)}), bf16[8,32,128]{2,0,1:T(8,128)(2,1)S(1)}, u32[]{:S(2)}, u32[]{:S(2)}) async-start(bf16[8,32,128]{2,0,1:T(8,128)(2,1)} %bitcast), calls=%async_computation | async-start | bytes 131072 | tf_op jit(solution)/shard_map/all_to_all | solution.py:103
  85.3 16.9 %all-to-all-start.1 = ((f32[32,1,256]{2,1,0:T(1,128)}), f32[32,1,256]{2,1,0:T(1,128)S(1)}, u32[]{:S(2)}, u32[]{:S(2)}) async-start(f32[32,1,256]{2,1,0:T(1,128)} %reshape.205), calls=%async_computation.1 | async-start | bytes 65536 | tf_op jit(solution)/shard_map/all_to_all | solution.py:20
  92.3 39.9 %copy-start.1 = (bf16[128,4096]{1,0:T(8,128)(2,1)S(1)}, bf16[128,4096]{1,0:T(8,128)(2,1)}, u32[]{:S(2)}) copy-start(bf16[128,4096]{1,0:T(8,128)(2,1)} %param.23) | copy-start | bytes 3145732
  104.4 13.7 %all-to-all-start.3 = ((f32[32,1,256]{2,1,0:T(1,128)}), f32[32,1,256]{2,1,0:T(1,128)S(1)}, u32[]{:S(2)}, u32[]{:S(2)}) async-start(f32[32,1,256]{2,1,0:T(1,128)} %reshape.207), calls=%async_computation.3 | async-start | bytes 65536 | tf_op jit(solution)/shard_map/all_to_all | solution.py:20
  118.1 14.0 %all-to-all-start.2 = ((bf16[32,8,128]{2,1,0:T(8,128)(2,1)}), bf16[32,8,128]{2,1,0:T(8,128)(2,1)S(1)}, u32[]{:S(2)}, u32[]{:S(2)}) async-start(bf16[32,8,128]{2,1,0:T(8,128)(2,1)} %fusion.25), calls=%async_computation.2 | async-start | bytes 131072 | tf_op jit(solution)/shard_map/all_to_all | solution.py:38
  146.9 13.7 %all-to-all-start.5 = ((f32[32,1,8]{2,1,0:T(1,128)}), f32[32,1,8]{2,1,0:T(1,128)S(1)}, u32[]{:S(2)}, u32[]{:S(2)}) async-start(f32[32,1,8]{2,1,0:T(1,128)} %broadcast_in_dim.83), calls=%async_computation.5 | async-start | bytes 32768 | tf_op jit(solution)/shard_map/all_to_all | solution.py:20
